TPU v7x, 32 devices: a whole 2x2x4 slice. The times are simulated.
32 devices in a mesh: cp: 8 (over y, x, core), tp: 4 (over z).
Axes of the slice: x: 2, y: 2, z: 4, core: 2. Of those that a mesh axis runs over, the one named last changes fastest.
Arguments:
- hidden: bfloat16 [2048, 4096], P('cp', 'tp'), may hold values from -120 to 120
- query_weight: bfloat16 [4096, 4096], P(None, 'tp'), may hold values from -0.1875 to 0.1875
- key_matrix: bfloat16 [4096, 512], P(None, 'tp'), may hold values from -0.09375 to 0.09375
- value_matrix: bfloat16 [4096, 512], P(None, 'tp'), may hold values from -0.09375 to 0.09375
- output_weight: bfloat16 [4096, 4096], P('tp'), may hold values from -0.1875 to 0.1875
- document_bounds: int32 [9], replicated, may hold values from 0 to 2048, as said below
- block_owner: int32 [16], replicated, may hold values from 0 to 7, as said below
Outputs:
- attended: bfloat16 [2048, 4096], P('cp', 'tp')
Inputs may be any that keep to these rules, and one draw needn't show every extreme that they name: document_bounds[0] = 0, document_bounds[8] = 2048, strictly rising; document i holds the tokens from document_bounds[i] to document_bounds[i + 1] - 1. `block_owner`: every index of cp is named by exactly 2 blocks.
All inputs are finite; a program needn't handle non-finite values.
Results may differ from a plain program's by a relative error of at most 0.012.
The roundings to bfloat16 on the way count: a program that leaves them out, or rounds other values in their place, can miss the bound.
Values may be sent and summed in bfloat16 or wider, within the bound.
A program may use at most 128 MiB of HBM per device.

v0:
```python
import math
import jax
import jax.numpy as jnp
from jax import lax
from jax.sharding import PartitionSpec as P

HEAD_WIDTH = 128
BLOCK = 128
rope_theta = 500000.0
rope_factor = 8.0
rope_context = 8192.0
masked_score = -1e30


def rope_inverse(head_size):
    halves = jnp.arange(head_size // 2, dtype=jnp.float32)
    inverse = 1.0 / rope_theta ** (2.0 * halves / head_size)
    wavelength = 2.0 * math.pi / inverse
    smooth = (rope_context / wavelength - 1.0) / 3.0
    blended = (1.0 - smooth) * inverse / rope_factor + smooth * inverse
    longer = jnp.where(wavelength > rope_context, inverse / rope_factor, blended)
    return jnp.where(wavelength < rope_context / 4.0, inverse, longer)


def document_of(tokens, bounds):
    inner_bounds = bounds[1:-1]
    return jnp.sum((tokens[:, None] >= inner_bounds[None, :]).astype(jnp.int32), axis=1)


def position_of(tokens, bounds):
    starts = bounds[:-1]
    document_start = jnp.max(
        jnp.where(starts[None, :] <= tokens[:, None], starts[None, :], 0), axis=1
    )
    return tokens - document_start


def rotate(raw_rows, tokens, bounds, head_size):
    row_count = raw_rows.shape[0]
    head_count = raw_rows.shape[1] // head_size
    angles = (
        position_of(tokens, bounds).astype(jnp.float32)[:, None] * rope_inverse(head_size)[None, :]
    )
    cosine = jnp.cos(angles)[:, None, :]
    sine_table = jnp.sin(angles)[:, None, :]
    heads_view = raw_rows.reshape(row_count, head_count, head_size)
    front_half = heads_view[:, :, : head_size // 2]
    back_half = heads_view[:, :, head_size // 2 :]
    turned = jnp.concatenate(
        [
            front_half * cosine - back_half * sine_table,
            back_half * cosine + front_half * sine_table,
        ],
        axis=2,
    )
    return turned.reshape(row_count, head_count * head_size).astype(jnp.bfloat16)


def owner_order(block_owner, per_device):
    block_count = block_owner.shape[0]
    blocks = jnp.arange(block_count, dtype=jnp.int32)
    same_owner = block_owner[:, None] == block_owner[None, :]
    earlier = blocks[None, :] < blocks[:, None]
    owner_rank = jnp.sum((same_owner & earlier).astype(jnp.int32), axis=1)
    target = block_owner * per_device + owner_rank
    return jnp.sum(jnp.where(target[None, :] == blocks[:, None], blocks[None, :], 0), axis=1)


def relayout(local_rows, block_order):
    cp_size = lax.axis_size("cp")
    row_count, row_width = local_rows.shape
    per_device = row_count // BLOCK
    portion = BLOCK // cp_size
    pieces = local_rows.reshape(per_device, cp_size, portion * row_width)
    spread = lax.all_to_all(pieces, "cp", split_axis=1, concat_axis=0, tiled=True)
    spread = spread.reshape(per_device * cp_size, portion * row_width)
    wanted = block_order.reshape(cp_size, per_device).T.reshape(-1)
    outgoing = jnp.take(spread, wanted, axis=0).reshape(per_device, cp_size, portion * row_width)
    arrived = lax.all_to_all(outgoing, "cp", split_axis=1, concat_axis=1, tiled=True)
    return arrived.reshape(row_count, row_width)


def project(local_rows, query_weight, key_matrix, value_matrix):
    weight_list = (query_weight, key_matrix, value_matrix)
    portion = lax.all_gather(local_rows, "tp", axis=1, tiled=True)
    return tuple(
        (jnp.dot(portion, weight, preferred_element_type=jnp.float32) for weight in weight_list)
    )


def attend(queries, query_tokens, key_rows, value_rows, key_tokens, bounds, head_size, kv_heads):
    row_count = queries.shape[0]
    query_group_width = queries.shape[1] // (kv_heads * head_size)
    grouped = queries.reshape(row_count, kv_heads, query_group_width, head_size).transpose(
        1, 2, 0, 3
    )
    grouped = grouped.reshape(kv_heads, query_group_width * row_count, head_size)
    query_documents = document_of(query_tokens, bounds)
    score_scale = 1.0 / math.sqrt(head_size)

    def update(flash_state, key_block, value_block, token_block):
        block_rows = key_block.shape[0]
        key_documents = document_of(token_block, bounds)
        allowed = (query_documents[:, None] == key_documents[None, :]) & (
            token_block[None, :] <= query_tokens[:, None]
        )
        running_max, running_sum, running_out = flash_state
        per_head_keys = key_block.reshape(block_rows, kv_heads, head_size).transpose(1, 0, 2)
        per_head_values = value_block.reshape(block_rows, kv_heads, head_size).transpose(1, 0, 2)
        scores = (
            jnp.einsum("khd,ksd->khs", grouped, per_head_keys, preferred_element_type=jnp.float32)
            * score_scale
        )
        wide_mask = jnp.tile(allowed, (query_group_width, 1))[None, :, :]
        scores = jnp.where(wide_mask, scores, masked_score)
        new_max = jnp.maximum(running_max, jnp.max(scores, axis=2))
        weights = jnp.where(wide_mask, jnp.exp(scores - new_max[:, :, None]), 0.0)
        factor = jnp.exp(running_max - new_max)
        new_sum = running_sum * factor + jnp.sum(weights, axis=2)
        new_out = running_out * factor[:, :, None] + jnp.einsum(
            "khs,ksd->khd",
            weights.astype(jnp.bfloat16),
            per_head_values,
            preferred_element_type=jnp.float32,
        )
        return (new_max, new_sum, new_out)

    initial = (
        jnp.full((kv_heads, query_group_width * row_count), masked_score, jnp.float32),
        jnp.zeros((kv_heads, query_group_width * row_count), jnp.float32),
        jnp.zeros((kv_heads, query_group_width * row_count, head_size), jnp.float32),
    )
    key_part = lax.all_gather(key_rows, "cp", axis=0, tiled=True)
    value_part = lax.all_gather(value_rows, "cp", axis=0, tiled=True)
    token_part = lax.all_gather(key_tokens, "cp", axis=0, tiled=True)
    part_rows = key_part.shape[0]
    block_rows = math.gcd(part_rows, 512)

    def one_block(block_index, inner_state):
        first_row = block_index * block_rows
        return update(
            inner_state,
            lax.dynamic_slice_in_dim(key_part, first_row, block_rows, 0),
            lax.dynamic_slice_in_dim(value_part, first_row, block_rows, 0),
            lax.dynamic_slice_in_dim(token_part, first_row, block_rows, 0),
        )

    final_max, final_sum, final_out = lax.fori_loop(0, part_rows // block_rows, one_block, initial)
    normalized = final_out / final_sum[:, :, None]
    merged = normalized.reshape(kv_heads, query_group_width, row_count, head_size).transpose(
        2, 0, 1, 3
    )
    return merged.reshape(row_count, kv_heads * query_group_width * head_size).astype(jnp.bfloat16)


def output_rows(heads_out, output_weight):
    head_terms = jnp.dot(heads_out, output_weight, preferred_element_type=jnp.float32)
    return lax.psum_scatter(head_terms.astype(jnp.bfloat16), "tp", scatter_dimension=1, tiled=True)


def local(
    hidden, query_weight, key_matrix, value_matrix, output_weight, document_bounds, block_owner
):
    cp_index = lax.axis_index("cp")
    row_count = hidden.shape[0]
    per_device = row_count // BLOCK
    block_order = owner_order(block_owner, per_device)
    own_blocks = lax.dynamic_slice_in_dim(block_order, cp_index * per_device, per_device, 0)
    new_tokens = (
        own_blocks[:, None] * BLOCK + jnp.arange(BLOCK, dtype=jnp.int32)[None, :]
    ).reshape(-1)
    kv_heads = key_matrix.shape[1] // HEAD_WIDTH
    moved = relayout(hidden, block_order)
    query_raw, key_raw, value_raw = project(moved, query_weight, key_matrix, value_matrix)
    queries = rotate(query_raw, new_tokens, document_bounds, HEAD_WIDTH)
    key_rows = rotate(key_raw, new_tokens, document_bounds, HEAD_WIDTH)
    value_rows = value_raw.astype(jnp.bfloat16)
    heads_out = attend(
        queries, new_tokens, key_rows, value_rows, new_tokens, document_bounds, HEAD_WIDTH, kv_heads
    )
    return output_rows(heads_out, output_weight)


def solution(mesh):
    placed = (P("cp", "tp"), P(None, "tp"), P(None, "tp"), P(None, "tp"), P("tp", None), P(), P())
    return jax.shard_map(
        local, mesh=mesh, in_specs=placed, out_specs=P("cp", "tp"), check_vma=False
    )
```

profile of v0, /device:TPU:0, one launch (start us, length us, event | category | flops | bytes accessed | tf_op | source)
XLA Modules:
  0.0 201.7 jit_solution(1744247314047454510)
XLA Ops:
  6.5 1.4 reshape.365
  7.9 1.3 copy.37
  9.2 5.2 %all-to-all-start = ((bf16[2,8,16384]{2,0,1:T(2,128)(2,1)}), bf16[2,8,16384]{2,0,1:T(2,128)(2,1)S(1)}, u32[]{:S(2)}, u32[]{:S(2)}) async-start(bf16[2,8,16384]{2,0,1:T(2,128)(2,1)} %copy.37), calls=%async_computation | async-start | bytes 1048576 | tf_op jit(solution)/shard_map/all_to_all | solution.py:75
  14.5 0.9 convert_reduce_fusion.2
  15.4 0.7 multiply_add_fusion
  16.1 0.1 select_reduce_fusion.1
  16.2 0.1 reshape.364
  16.3 0.1 copy.38
  16.3 0.1 reshape.367
  16.5 7.7 %all-to-all-done = bf16[2,8,16384]{2,0,1:T(2,128)(2,1)S(1)} async-done(((bf16[2,8,16384]{2,0,1:T(2,128)(2,1)}), bf16[2,8,16384]{2,0,1:T(2,128)(2,1)S(1)}, u32[]{:S(2)}, u32[]{:S(2)}) %all-to-all-start) | async-done | bytes 524320 | tf_op jit(solution)/shard_map/all_to_all | solution.py:75
  24.2 0.2 reshape.366
  24.4 0.9 gather_fusion
  25.3 0.9 broadcast_select_fusion.2
  26.2 12.1 %all_to_all.20 = bf16[2,8,16384]{2,0,1:T(2,128)(2,1)S(1)} all-to-all(bf16[2,8,16384]{2,0,1:T(2,128)(2,1)S(1)} %broadcast_select_fusion.2), channel_id=1, replica_groups=mesh['cp'=8,'tp'=4] {'cp'}, dimensions={1} | all-to-all | bytes 1048576 | tf_op jit(solution)/shard_map/all_to_all | solution.py:79
  38.3 0.3 copy.40
  38.6 1.0 reshape.368
  40.0 8.0 %all-gather.1 = s32[8,1,256]{2,1,0:T(1,128)S(1)} all-gather(s32[1,1,256]{2,1,0:T(1,128)S(1)} %bitcast.115), channel_id=1, replica_groups=mesh['cp'=8,'tp'=4] {'cp'}, dimensions={0}, use_global_device_ids=true | all-gather | bytes 9216 | tf_op jit(solution)/shard_map/all_gather | solution.py:135
  48.0 0.1 convert_reduce_fusion.1
  48.0 0.1 select_reduce_fusion
  48.2 0.5 multiply_cosine_fusion
  48.7 36.1 %all-gather.4.cloned.1.call-done = bf16[256,4096]{1,0:T(8,128)(2,1)} async-done(((bf16[256,1024]{1,0:T(8,128)(2,1)}), bf16[256,4096]{1,0:T(8,128)(2,1)}) %all-gather.4.cloned.1.call-update) | async-done | bytes 2097168 | tf_op jit(solution)/shard_map/all_gather | solution.py:85
  84.8 2.4 %convolution_bitcast_fusion.2 = f32[256,1,128]{0,2,1:T(8,128)S(1)} fusion(bf16[256,4096]{1,0:T(8,128)(2,1)} %all-gather.4.cloned.1.call-done, bf16[4096,128]{1,0:T(8,128)(2,1)S(1)} %copy-done), kind=kOutput, calls=%fused_computation.34 | convolution fusion | flops 268435456 | bytes 3276800 | tf_op jit(solution)/shard_map/dot_general | solution.py:87
  87.3 0.3 fusion.30
  87.6 6.3 %convolution_bitcast_fusion.1 = f32[32,8,8,128]{3,1,2,0:T(8,128)S(1)} fusion(bf16[256,4096]{1,0:T(8,128)(2,1)} %all-gather.4.cloned.1.call-done, bf16[4096,1024]{1,0:T(8,128)(2,1)} %param.10), kind=kOutput, calls=%fused_computation.33 | convolution fusion | flops 2147483648 | bytes 11534336 | tf_op jit(solution)/shard_map/dot_general | solution.py:87
  94.0 0.2 copy.46
  94.2 0.5 fusion.23
  94.7 0.3 maximum_bitcast_fusion
  95.0 0.9 copy.41
  95.9 10.9 %all-gather = bf16[2048,1,128]{0,2,1:T(8,128)(2,1)S(1)} all-gather(bf16[256,1,128]{0,2,1:T(8,128)(2,1)S(1)} %pad_maximum_fusion), channel_id=2, replica_groups=mesh['cp'=8,'tp'=4] {'cp'}, dimensions={0}, use_global_device_ids=true | all-gather | bytes 589824 | tf_op jit(solution)/shard_map/all_gather | solution.py:133
  106.7 0.7 convolution_convert_fusion.1
  107.4 10.0 %all_gather.15 = bf16[2048,128]{1,0:T(8,128)(2,1)S(1)} all-gather(bf16[256,128]{1,0:T(8,128)(2,1)S(1)} %convolution_convert_fusion.1), channel_id=1, replica_groups=mesh['cp'=8,'tp'=4] {'cp'}, dimensions={0}, use_global_device_ids=true | all-gather | bytes 589824 | tf_op jit(solution)/shard_map/all_gather | solution.py:134
  117.4 28.0 %while.18 = (s32[]{:T(128)}, f32[1,2048]{1,0:T(1,128)S(1)}, f32[1,2048]{1,0:T(1,128)S(1)}, f32[1,2048,128]{2,1,0:T(8,128)S(1)}, s32[256]{0:T(256)S(1)}, /*index=...) while((s32[]{:T(128)}, f32[1,2048]{1,0:T(1,128)S(1)}, ...), condition=%wide.region_8.9_spmd.clone, body=%wide.region_4.8_spmd.clone.sunk | while | flops 551702784 | bytes 22166840 | solution.py:148
  117.7 0.1 convert_reduce_fusion.4
  117.7 0.2 compare_and_fusion.3
  118.0 0.5 tile.22
  118.4 0.6 copy.49
  119.1 2.0 fusion.53
  121.1 1.2 fusion.55
  122.4 2.0 %fusion.57 = f32[1,2048,128]{2,1,0:T(8,128)S(1)} fusion(pred[2048,512]{0,1:T(8,128)(4,1)S(1)} %bitcast.98, f32[512,2048]{1,0:T(8,128)S(1)} %get-tuple-element.403, f32[2048]{0:T(1024)S(1)} %bitcast.102, f32[1,2048,128]{2,1,0:T(8,128)S(1)} %get-tuple-element.424, f32[2048]{0:T(1024)S(1)} %bitcast.111, pred[]{:T(512)S(6)} %compare.3, ...), kind=kOutput, calls=%fused_computation.8.clone.1 | convolution fusion | flops 274464768 | bytes 7487493 | tf_op jit(solution)/shard_map/while/body/eval_jaxpr/khs,ksd->khd/dot_general | solution.py:120
  124.7 0.1 convert_reduce_fusion.4
  124.8 0.2 compare_and_fusion.3
  125.0 0.5 tile.22
  125.5 0.6 copy.49
  126.1 2.0 fusion.53
  128.1 1.2 fusion.55
  129.4 2.1 %fusion.57 = f32[1,2048,128]{2,1,0:T(8,128)S(1)} fusion(pred[2048,512]{0,1:T(8,128)(4,1)S(1)} %bitcast.98, f32[512,2048]{1,0:T(8,128)S(1)} %get-tuple-element.403, f32[2048]{0:T(1024)S(1)} %bitcast.102, f32[1,2048,128]{2,1,0:T(8,128)S(1)} %get-tuple-element.424, f32[2048]{0:T(1024)S(1)} %bitcast.111, pred[]{:T(512)S(6)} %compare.3, ...), kind=kOutput, calls=%fused_computation.8.clone.1 | convolution fusion | flops 274464768 | bytes 7487493 | tf_op jit(solution)/shard_map/while/body/eval_jaxpr/khs,ksd->khd/dot_general | solution.py:120
  131.7 0.1 convert_reduce_fusion.4
  131.8 0.2 compare_and_fusion.3
  132.0 0.5 tile.22
  132.5 0.6 copy.49
  133.1 2.0 fusion.53
  135.1 1.2 fusion.55
  136.4 2.0 %fusion.57 = f32[1,2048,128]{2,1,0:T(8,128)S(1)} fusion(pred[2048,512]{0,1:T(8,128)(4,1)S(1)} %bitcast.98, f32[512,2048]{1,0:T(8,128)S(1)} %get-tuple-element.403, f32[2048]{0:T(1024)S(1)} %bitcast.102, f32[1,2048,128]{2,1,0:T(8,128)S(1)} %get-tuple-element.424, f32[2048]{0:T(1024)S(1)} %bitcast.111, pred[]{:T(512)S(6)} %compare.3, ...), kind=kOutput, calls=%fused_computation.8.clone.1 | convolution fusion | flops 274464768 | bytes 7487493 | tf_op jit(solution)/shard_map/while/body/eval_jaxpr/khs,ksd->khd/dot_general | solution.py:120
  138.7 0.1 convert_reduce_fusion.4
  138.8 0.2 compare_and_fusion.3
  139.0 0.5 tile.22
  139.5 0.6 copy.49
  140.1 2.0 fusion.53
  142.1 1.2 fusion.55
  143.4 2.1 %fusion.57 = f32[1,2048,128]{2,1,0:T(8,128)S(1)} fusion(pred[2048,512]{0,1:T(8,128)(4,1)S(1)} %bitcast.98, f32[512,2048]{1,0:T(8,128)S(1)} %get-tuple-element.403, f32[2048]{0:T(1024)S(1)} %bitcast.102, f32[1,2048,128]{2,1,0:T(8,128)S(1)} %get-tuple-element.424, f32[2048]{0:T(1024)S(1)} %bitcast.111, pred[]{:T(512)S(6)} %compare.3, ...), kind=kOutput, calls=%fused_computation.8.clone.1 | convolution fusion | flops 274464768 | bytes 7487493 | tf_op jit(solution)/shard_map/while/body/eval_jaxpr/khs,ksd->khd/dot_general | solution.py:120
  145.5 0.3 divide_convert_fusion
  145.8 0.2 copy.43
  146.1 7.1 %convolution_convert_fusion = bf16[256,4096]{1,0:T(8,128)(2,1)} fusion(bf16[256,1024]{0,1:T(8,128)(2,1)S(1)} %bitcast.103, bf16[1024,4096]{1,0:T(8,128)(2,1)} %param.13), kind=kOutput, calls=%fused_computation.32 | convolution fusion | flops 2148532224 | bytes 11010048 | tf_op jit(solution)/shard_map/dot_general | solution.py:157
  153.2 41.7 %reduce-scatter.2.cloned.1.call-done = bf16[256,1024]{1,0:T(8,128)(2,1)} async-done(((bf16[256,4096]{1,0:T(8,128)(2,1)}), bf16[256,1024]{1,0:T(8,128)(2,1)}) %reduce-scatter.2.cloned.1.call-update) | async-done | bytes 524304 | tf_op jit(solution)/shard_map/reduce_scatter | solution.py:158
  (48 shorter events, 1.6 us)
Async XLA Ops:
  6.5 78.3 %copy-start = (bf16[4096,128]{1,0:T(8,128)(2,1)S(1)}, bf16[4096,128]{1,0:T(8,128)(2,1)}, u32[]{:S(2)}) copy-start(bf16[4096,128]{1,0:T(8,128)(2,1)} %param.11) | copy-start | bytes 3145732
  9.2 14.9 %all-to-all-start = ((bf16[2,8,16384]{2,0,1:T(2,128)(2,1)}), bf16[2,8,16384]{2,0,1:T(2,128)(2,1)S(1)}, u32[]{:S(2)}, u32[]{:S(2)}) async-start(bf16[2,8,16384]{2,0,1:T(2,128)(2,1)} %copy.37), calls=%async_computation | async-start | bytes 1048576 | tf_op jit(solution)/shard_map/all_to_all | solution.py:75
  14.4 70.4 %all-gather.4.cloned.1.call-start = ((), (), s32[]{:S(2)}) async-start(), calls=%async_computation.3 | async-start | bytes 2621440 | tf_op jit(solution)/shard_map/all_gather | solution.py:85
  24.4 15.4 %copy-start.3 = (s32[9]{0:T(128)S(1)}, s32[9]{0:T(128)}, u32[]{:S(2)}) copy-start(s32[9]{0:T(128)} %param.14) | copy-start | bytes 112
  39.7 155.2 %reduce-scatter.2.cloned.1.call-start = ((), (), s32[]{:S(2)}) async-start(), calls=%async_computation.4 | async-start | bytes 2621440 | tf_op jit(solution)/shard_map/reduce_scatter | solution.py:158
  93.9 12.8 %copy-start.1 = (bf16[256,4096]{1,0:T(8,128)(2,1)S(1)}, bf16[256,4096]{1,0:T(8,128)(2,1)}, u32[]{:S(2)}) copy-start(bf16[256,4096]{1,0:T(8,128)(2,1)} %all-gather.4.cloned.1.call-done) | copy-start | bytes 6291460
  93.9 12.8 %copy-start.2 = (bf16[4096,128]{1,0:T(8,128)(2,1)S(1)}, bf16[4096,128]{1,0:T(8,128)(2,1)}, u32[]{:S(2)}) copy-start(bf16[4096,128]{1,0:T(8,128)(2,1)} %param.12) | copy-start | bytes 3145732
Sparse Core Ops, SparseCore 0:
  39.8 45.0 all-gather.3
  153.3 41.4 reduce-scatter.1
where the time goes:
time: 202 us
  waiting for transfers between devices  85.5 us (42%)
  blocking collectives  40.9 us (20%)
  matrix products  32.6 us (16%)
  between operations  13.6 us (7%)
  local copies, waits for them, and re-layouts  11.8 us (6%)
  other arithmetic  11.7 us (6%)
  starting transfers between devices  5.28 us (3%)
    reduce_scatter x1, waiting for transfers between devices, output_rows(): lax.psum_scatter(head_terms.astype(jnp.bfloat16), 'tp', scatter_dimension...  41.7 us
    all_gather x1, waiting for transfers between devices, project(): portion = lax.all_gather(local_rows, 'tp', axis=1, tiled=True)  36.1 us
    all_to_all x1, blocking collectives, relayout(): lax.all_to_all(outgoing, 'cp', split_axis=1, concat_axis=1, tiled=True)  12.1 us
    all_gather x1, blocking collectives, attend(): key_part = lax.all_gather(key_rows, 'cp', axis=0, tiled=True)  10.9 us
    all_gather x1, blocking collectives, attend(): value_part = lax.all_gather(value_rows, 'cp', axis=0, tiled=True)  9.99 us
    dot_general x3, matrix products, project(): jnp.dot(portion, weight, preferred_element_type=jnp.float32)  9.46 us
    dot_general x4, matrix products, update(): jnp.einsum('khs,ksd->khd', weights.astype(jnp.bfloat16), per_head_values,...  8.2 us
    all_gather x1, blocking collectives, attend(): token_part = lax.all_gather(key_tokens, 'cp', axis=0, tiled=True)  7.96 us
  transfers between devices with their start and end apart: 3, of which 3 were waited for; matrix products, arithmetic and copies ran while one was open for 1% of the time, Pallas kernels for 0%

commit v1 on v0

--- a/solution.py
+++ b/solution.py
@@ -72,7 +72,10 @@
     per_device = row_count // BLOCK
     portion = BLOCK // cp_size
     pieces = local_rows.reshape(per_device, cp_size, portion * row_width)
-    spread = lax.all_to_all(pieces, "cp", split_axis=1, concat_axis=0, tiled=True)
+    spread = jnp.concatenate(
+        lax.all_to_all(jnp.stack(jnp.split(pieces, lax.axis_size("cp"), axis=1)), "cp", 0, 0),
+        axis=0,
+    )
     spread = spread.reshape(per_device * cp_size, portion * row_width)
     wanted = block_order.reshape(cp_size, per_device).T.reshape(-1)
     outgoing = jnp.take(spread, wanted, axis=0).reshape(per_device, cp_size, portion * row_width)

time: 202 us -> 208 us (1.030)
  local copies, waits for them, and re-layouts: 11.8 us -> 17.5 us
    unnamed x9 -> x18, local copies, waits for them, and re-layouts: 0.22 us -> 5.35 us
where the time goes in v1:
time: 208 us; the launch traced here: 207 us
  waiting for transfers between devices  86.8 us (42%)
  blocking collectives  40.9 us (20%)
  matrix products  32.6 us (16%)
  local copies, waits for them, and re-layouts  17.5 us (8%)
  between operations  13.6 us (7%)
  other arithmetic  10.3 us (5%)
  starting transfers between devices  5.28 us (3%)
    reduce_scatter x1, waiting for transfers between devices, output_rows(): lax.psum_scatter(head_terms.astype(jnp.bfloat16), 'tp', scatter_dimension...  41.7 us
    all_gather x1, waiting for transfers between devices, project(): portion = lax.all_gather(local_rows, 'tp', axis=1, tiled=True)  36.1 us
    all_to_all x1, blocking collectives, relayout(): lax.all_to_all(outgoing, 'cp', split_axis=1, concat_axis=1, tiled=True)  12.1 us
    all_gather x1, blocking collectives, attend(): key_part = lax.all_gather(key_rows, 'cp', axis=0, tiled=True)  10.9 us
    all_gather x1, blocking collectives, attend(): value_part = lax.all_gather(value_rows, 'cp', axis=0, tiled=True)  9.99 us
    dot_general x3, matrix products, project(): jnp.dot(portion, weight, preferred_element_type=jnp.float32)  9.45 us
    all_to_all x1, waiting for transfers between devices, relayout(): lax.all_to_all(jnp.stack(jnp.split(pieces, lax.axis_size('cp'), axis=1)),...  9.06 us
    dot_general x4, matrix products, update(): jnp.einsum('khs,ksd->khd', weights.astype(jnp.bfloat16), per_head_values,...  8.2 us
  transfers between devices with their start and end apart: 3, of which 3 were waited for; matrix products, arithmetic and copies ran while one was open for 1% of the time, Pallas kernels for 0%

profile of v1, /device:TPU:0, one launch (start us, length us, event | category | flops | bytes accessed | tf_op | source)
XLA Modules:
  0.0 207.4 jit_solution(3317377636567359963)
XLA Ops:
  6.5 1.4 reshape.361
  7.9 1.1 fusion.36
  9.1 0.7 bitcast_dynamic-update-slice_fusion.7
  9.8 0.7 bitcast_dynamic-update-slice_fusion.6
  10.5 0.7 bitcast_dynamic-update-slice_fusion.5
  11.3 0.7 bitcast_dynamic-update-slice_fusion.4
  12.0 0.7 bitcast_dynamic-update-slice_fusion.3
  12.7 0.7 bitcast_dynamic-update-slice_fusion.2
  13.5 0.7 bitcast_dynamic-update-slice_fusion.1
  14.2 0.7 bitcast_dynamic-update-slice_fusion
  14.9 5.2 %all-to-all-start = ((bf16[8,2,1,16384]{3,1,2,0:T(2,128)(2,1)}), bf16[8,2,1,16384]{3,1,2,0:T(2,128)(2,1)S(1)}, u32[]{:S(2)}, u32[]{:S(2)}) async-start(bf16[8,2,1,16384]{3,1,2,0:T(2,128)(2,1)} %bitcast_dynamic-update-slice_fusion), calls=%async_computation | async-start | bytes 1048576 | tf_op jit(solution)/shard_map/all_to_all | solution.py:76
  20.2 0.2 convert_reduce_fusion.2
  20.4 0.1 select_reduce_fusion.1
  20.8 9.1 %all-to-all-done = bf16[8,2,1,16384]{3,1,2,0:T(2,128)(2,1)S(1)} async-done(((bf16[8,2,1,16384]{3,1,2,0:T(2,128)(2,1)}), bf16[8,2,1,16384]{3,1,2,0:T(2,128)(2,1)S(1)}, u32[]{:S(2)}, u32[]{:S(2)}) %all-to-all-start) | async-done | bytes 524320 | tf_op jit(solution)/shard_map/all_to_all | solution.py:76
  29.8 0.2 reshape_reshape.3
  30.0 0.9 gather_fusion
  30.9 0.9 broadcast_select_fusion.2
  31.8 12.1 %all_to_all.10 = bf16[2,8,16384]{2,0,1:T(2,128)(2,1)S(1)} all-to-all(bf16[2,8,16384]{2,0,1:T(2,128)(2,1)S(1)} %broadcast_select_fusion.2), channel_id=1, replica_groups=mesh['cp'=8,'tp'=4] {'cp'}, dimensions={1} | all-to-all | bytes 1048576 | tf_op jit(solution)/shard_map/all_to_all | solution.py:82
  44.0 0.3 copy.134
  44.3 1.0 reshape.363
  45.6 8.0 %all-gather.1 = s32[8,1,256]{2,1,0:T(1,128)S(1)} all-gather(s32[1,1,256]{2,1,0:T(1,128)S(1)} %bitcast.127), channel_id=1, replica_groups=mesh['cp'=8,'tp'=4] {'cp'}, dimensions={0}, use_global_device_ids=true | all-gather | bytes 9216 | tf_op jit(solution)/shard_map/all_gather | solution.py:138
  53.9 0.5 multiply_cosine_fusion
  54.4 36.1 %all-gather.4.cloned.1.call-done = bf16[256,4096]{1,0:T(8,128)(2,1)} async-done(((bf16[256,1024]{1,0:T(8,128)(2,1)}), bf16[256,4096]{1,0:T(8,128)(2,1)}) %all-gather.4.cloned.1.call-update) | async-done | bytes 2097168 | tf_op jit(solution)/shard_map/all_gather | solution.py:88
  90.5 2.4 %convolution_bitcast_fusion.2 = f32[256,1,128]{0,2,1:T(8,128)S(1)} fusion(bf16[256,4096]{1,0:T(8,128)(2,1)} %all-gather.4.cloned.1.call-done, bf16[4096,128]{1,0:T(8,128)(2,1)S(1)} %copy-done), kind=kOutput, calls=%fused_computation.34 | convolution fusion | flops 268435456 | bytes 3276800 | tf_op jit(solution)/shard_map/dot_general | solution.py:90
  92.9 0.3 fusion.30
  93.3 6.3 %convolution_bitcast_fusion.1 = f32[32,8,8,128]{3,1,2,0:T(8,128)S(1)} fusion(bf16[256,4096]{1,0:T(8,128)(2,1)} %all-gather.4.cloned.1.call-done, bf16[4096,1024]{1,0:T(8,128)(2,1)} %param.10), kind=kOutput, calls=%fused_computation.33 | convolution fusion | flops 2147483648 | bytes 11534336 | tf_op jit(solution)/shard_map/dot_general | solution.py:90
  99.6 0.2 copy.148
  99.8 0.5 fusion.23
  100.4 0.3 maximum_bitcast_fusion
  100.7 0.9 copy.135
  101.5 10.9 %all-gather = bf16[2048,1,128]{0,2,1:T(8,128)(2,1)S(1)} all-gather(bf16[256,1,128]{0,2,1:T(8,128)(2,1)S(1)} %pad_maximum_fusion), channel_id=2, replica_groups=mesh['cp'=8,'tp'=4] {'cp'}, dimensions={0}, use_global_device_ids=true | all-gather | bytes 589824 | tf_op jit(solution)/shard_map/all_gather | solution.py:136
  112.4 0.7 convolution_convert_fusion.1
  113.1 10.0 %all_gather.15 = bf16[2048,128]{1,0:T(8,128)(2,1)S(1)} all-gather(bf16[256,128]{1,0:T(8,128)(2,1)S(1)} %convolution_convert_fusion.1), channel_id=1, replica_groups=mesh['cp'=8,'tp'=4] {'cp'}, dimensions={0}, use_global_device_ids=true | all-gather | bytes 589824 | tf_op jit(solution)/shard_map/all_gather | solution.py:137
  123.1 28.0 %while.18 = (s32[]{:T(128)}, f32[1,2048]{1,0:T(1,128)S(1)}, f32[1,2048]{1,0:T(1,128)S(1)}, f32[1,2048,128]{2,1,0:T(8,128)S(1)}, s32[256]{0:T(256)S(1)}, /*index=...) while((s32[]{:T(128)}, f32[1,2048]{1,0:T(1,128)S(1)}, ...), condition=%wide.region_8.9_spmd.clone, body=%wide.region_4.8_spmd.clone.sunk | while | flops 551702784 | bytes 22166840 | solution.py:151
  123.3 0.1 convert_reduce_fusion.4
  123.4 0.2 compare_and_fusion.3
  123.6 0.5 tile.22
  124.1 0.6 copy.159
  124.8 2.0 fusion.54
  126.7 1.2 fusion.56
  128.0 2.0 fusion.58
  130.3 0.1 convert_reduce_fusion.4
  130.4 0.2 compare_and_fusion.3
  130.6 0.5 tile.22
  131.1 0.6 copy.159
  131.8 2.0 fusion.54
  133.8 1.2 fusion.56
  135.0 2.1 fusion.58
  137.4 0.2 compare_and_fusion.3
  137.7 0.5 tile.22
  138.1 0.6 copy.159
  138.8 2.0 fusion.54
  140.8 1.2 fusion.56
  142.1 2.0 fusion.58
  144.5 0.2 compare_and_fusion.3
  144.7 0.5 tile.22
  145.2 0.6 copy.159
  145.8 2.0 fusion.54
  147.8 1.2 fusion.56
  149.1 2.1 fusion.58
  151.2 0.3 divide_convert_fusion
  151.5 0.2 copy.137
  151.7 7.1 %convolution_convert_fusion = bf16[256,4096]{1,0:T(8,128)(2,1)} fusion(bf16[256,1024]{0,1:T(8,128)(2,1)S(1)} %bitcast.116, bf16[1024,4096]{1,0:T(8,128)(2,1)} %param.13), kind=kOutput, calls=%fused_computation.32 | convolution fusion | flops 2148532224 | bytes 11010048 | tf_op jit(solution)/shard_map/dot_general | solution.py:160
  158.9 41.7 %reduce-scatter.2.cloned.1.call-done = bf16[256,1024]{1,0:T(8,128)(2,1)} async-done(((bf16[256,4096]{1,0:T(8,128)(2,1)}), bf16[256,1024]{1,0:T(8,128)(2,1)}) %reduce-scatter.2.cloned.1.call-update) | async-done | bytes 524304 | tf_op jit(solution)/shard_map/reduce_scatter | solution.py:161
  (58 shorter events, 2.2 us)
Async XLA Ops:
  6.5 84.0 %copy-start = (bf16[4096,128]{1,0:T(8,128)(2,1)S(1)}, bf16[4096,128]{1,0:T(8,128)(2,1)}, u32[]{:S(2)}) copy-start(bf16[4096,128]{1,0:T(8,128)(2,1)} %param.11) | copy-start | bytes 3145732
  6.5 13.6 %copy-start.4 = (s32[16]{0:T(128)S(1)}, s32[16]{0:T(128)}, u32[]{:S(2)}) copy-start(s32[16]{0:T(128)} %param.15) | copy-start | bytes 196
  14.9 14.9 %all-to-all-start = ((bf16[8,2,1,16384]{3,1,2,0:T(2,128)(2,1)}), bf16[8,2,1,16384]{3,1,2,0:T(2,128)(2,1)S(1)}, u32[]{:S(2)}, u32[]{:S(2)}) async-start(bf16[8,2,1,16384]{3,1,2,0:T(2,128)(2,1)} %bitcast_dynamic-update-slice_fusion), calls=%async_computation | async-start | bytes 1048576 | tf_op jit(solution)/shard_map/all_to_all | solution.py:76
  20.1 70.4 %all-gather.4.cloned.1.call-start = ((), (), s32[]{:S(2)}) async-start(), calls=%async_computation.3 | async-start | bytes 2621440 | tf_op jit(solution)/shard_map/all_gather | solution.py:88
  30.0 15.4 %copy-start.3 = (s32[9]{0:T(128)S(1)}, s32[9]{0:T(128)}, u32[]{:S(2)}) copy-start(s32[9]{0:T(128)} %param.14) | copy-start | bytes 112
  45.3 155.2 %reduce-scatter.2.cloned.1.call-start = ((), (), s32[]{:S(2)}) async-start(), calls=%async_computation.4 | async-start | bytes 2621440 | tf_op jit(solution)/shard_map/reduce_scatter | solution.py:161
  99.6 12.8 %copy-start.1 = (bf16[256,4096]{1,0:T(8,128)(2,1)S(1)}, bf16[256,4096]{1,0:T(8,128)(2,1)}, u32[]{:S(2)}) copy-start(bf16[256,4096]{1,0:T(8,128)(2,1)} %all-gather.4.cloned.1.call-done) | copy-start | bytes 6291460
  99.6 12.8 %copy-start.2 = (bf16[4096,128]{1,0:T(8,128)(2,1)S(1)}, bf16[4096,128]{1,0:T(8,128)(2,1)}, u32[]{:S(2)}) copy-start(bf16[4096,128]{1,0:T(8,128)(2,1)} %param.12) | copy-start | bytes 3145732
Sparse Core Ops, SparseCore 0:
  45.4 45.0 all-gather.3
  159.0 41.4 reduce-scatter.1
